TPU v7x, 32 devices: a whole 2x2x4 slice. The times are simulated.
32 devices in a mesh: cfg: 8 (over z, y), lat: 4 (over x, core).
Axes of the slice: x: 2, y: 2, z: 4, core: 2. Of those that a mesh axis runs over, the one named last changes fastest.
Arguments:
- latent_mode: float32 [16, 131072], P('cfg', 'lat'), may hold values from -6 to 6
- latent_var: float32 [16, 131072], P('cfg', 'lat'), may hold values from 0.05 to 2
- config_weight: float32 [16], P('cfg'), may hold values from 0.05 to 20
- grid_offset: float32 [64], replicated, may hold values from -3 to 3
Outputs:
- marginal_density: float32 [64, 131072], P(None, ('cfg', 'lat'))
- marginal_moments: float32 [2, 131072], P(None, ('cfg', 'lat'))
All inputs are finite; a program needn't handle non-finite values.
Results may differ from a plain program's by a relative error of at most 0.00002.
Values sent between devices are 32-bit elements; how exact they have to be, the bound alone decides.
A program may use at most 64 MiB of HBM per device.

v0:
```python
import functools
import math

import jax
import jax.numpy as jnp
from jax import lax
from jax.experimental import pallas as pl
from jax.experimental.pallas import tpu as pltpu
from jax.sharding import PartitionSpec as P

LANES = 128
CORES = 2
FAR = 0
MESH = pl.DeviceIdType.MESH
HALF_LOG2E = 0.5 * math.log2(math.e)
TWO_PI = 6.283185307179586


def over(n, body, init):
    if n <= 16:
        for i in range(n):
            init = body(i, init)
        return init
    return lax.fori_loop(0, n, body, init)


def densities(grid_col, rows_u, rows_v, rows_c, out_ref, first):
    n_config, tiles, _ = rows_u.shape
    grid = grid_col[...]

    def one_tile(t, carry):
        def term(k, acc):
            at = grid * rows_u[k, pl.ds(t, 1), :] + rows_v[k, pl.ds(t, 1), :]
            return acc + jnp.exp2(rows_c[k, pl.ds(t, 1), :] - at * at)

        acc = over(n_config, term, jnp.zeros(grid.shape, jnp.float32))
        column_at = pl.multiple_of((first + t) * LANES, LANES)
        out_ref[:, pl.ds(column_at, LANES)] = acc
        return carry

    lax.fori_loop(0, tiles, one_tile, 0)


def kernel(
    n_cfg, n_lat, own, n_chunk, n_far, tiles,
    mode_ref, var_ref, weight_ref, grid_ref,
    density_ref, moments_ref, rows_u, rows_v, rows_c, grid_col,
    stage, relay, landed, weights, norm,
    load_sem, pass_sem, relay_sem, far_sem, send_sem, recv_sem, wsend_sem, wrecv_sem,
):
    my_cfg = lax.axis_index("cfg")
    my_lat = lax.axis_index("lat")
    me = my_cfg * n_lat + my_lat
    n_group = n_lat // CORES
    group, core = my_lat // CORES, lax.rem(my_lat, CORES)
    n_config = n_cfg * own
    per_group = n_cfg // n_group

    barrier = pltpu.get_barrier_semaphore()
    sender = group * CORES + lax.rem(me // n_cfg, CORES)

    def greet(i, carry):
        @pl.when(jnp.logical_or(i != my_cfg, sender != my_lat))
        def _():
            pl.semaphore_signal(
                barrier, inc=1, device_id=(i, sender), device_id_type=MESH
            )
        return carry

    for step in range(1, n_group):
        peer = lax.rem(group + step, n_group) * CORES + core
        pl.semaphore_signal(
            barrier, inc=1, device_id=(my_cfg, peer), device_id_type=MESH
        )
    over(n_cfg, greet, 0)
    waits = n_group - 1 + n_cfg
    if n_far:
        waits = waits + n_cfg - per_group
        origin_lat = me // n_cfg

        def greet_far(i, carry):
            @pl.when(origin_lat // CORES != group)
            def _():
                pl.semaphore_signal(
                    barrier, inc=1, device_id=(i, origin_lat), device_id_type=MESH
                )
            return carry

        over(n_cfg, greet_far, 0)


    for chunk in range(n_chunk):
        for step in list(range(1, n_group)) + [0]:
            to = lax.rem(group + step, n_group)
            for a, ref in enumerate((mode_ref, var_ref)):
                pltpu.make_async_copy(
                    ref.at[:, to, :, chunk], stage.at[to, chunk, :, :, a],
                    load_sem.at[step, chunk],
                ).start()

    keeps = (sender == my_lat).astype(jnp.int32)
    pl.semaphore_wait(barrier, waits - keeps)

    def loaded(step, chunk):
        to = lax.rem(group + step, n_group)
        block = stage.at[to, chunk]
        pltpu.make_async_copy(block, block, load_sem.at[step, chunk]).wait()

    n_a = n_cfg // n_lat
    n_part = 2 if n_a % 2 == 0 else 1
    size = n_a // n_part
    pieces = [(chunk, part) for chunk in range(n_chunk) for part in range(n_part)]
    passed = pieces[:len(pieces) - n_far] if n_far else pieces

    for chunk, part in pieces:
        for step in range(1, n_group):
            to = lax.rem(group + step, n_group)
            if part == 0:
                loaded(step, chunk)
            if (chunk, part) in passed:
                span = pl.ds(part * size, size)
                pltpu.make_async_remote_copy(
                    src_ref=stage.at[to, chunk, span],
                    dst_ref=relay.at[group, chunk, span],
                    send_sem=pass_sem.at[to, part],
                    recv_sem=relay_sem.at[group, chunk, part],
                    device_id=(my_cfg, to * CORES + core), device_id_type=MESH,
                ).start()

    def target(origin, i, to=group):
        slot = (i // CORES) * n_lat + to * CORES + i % CORES
        flat = (origin * CORES + core) * n_cfg + slot
        return flat, (flat // n_lat, lax.rem(flat, n_lat))

    def send_weights(origin):
        def send(i, carry):
            flat, device = target(origin, i)

            @pl.when(flat == me)
            def _():
                pltpu.make_async_copy(weight_ref, weights.at[my_cfg], wrecv_sem).start()

            @pl.when(flat != me)
            def _():
                pltpu.make_async_remote_copy(
                    src_ref=weight_ref, dst_ref=weights.at[my_cfg],
                    send_sem=wsend_sem.at[origin, i], recv_sem=wrecv_sem,
                    device_id=device, device_id_type=MESH,
                ).start()
            return carry

        over(per_group, send, 0)

    def send_blocks(origin, source, chunk, part):
        def send(i, carry):
            i = i + part * size * CORES
            flat, device = target(origin, i)
            src = source.at[i // CORES, i % CORES]
            dst = landed.at[chunk, my_cfg]

            @pl.when(flat == me)
            def _():
                pltpu.make_async_copy(src, dst, recv_sem.at[chunk]).start()

            @pl.when(flat != me)
            def _():
                pltpu.make_async_remote_copy(
                    src_ref=src, dst_ref=dst,
                    send_sem=send_sem.at[origin, i], recv_sem=recv_sem.at[chunk],
                    device_id=device, device_id_type=MESH,
                ).start()
            return carry

        over(size * CORES, send, 0)

    def send_far(step, chunk, part):
        to = lax.rem(group + step, n_group)

        def send(i, carry):
            i = i + part * size * CORES
            _, device = target(group, i, to)
            pltpu.make_async_remote_copy(
                src_ref=stage.at[to, chunk, i // CORES, i % CORES],
                dst_ref=landed.at[chunk, my_cfg],
                send_sem=far_sem.at[to, chunk, i], recv_sem=recv_sem.at[chunk],
                device_id=device, device_id_type=MESH,
            ).start()
            return carry

        over(size * CORES, send, 0)

    def send_own(chunk):
        loaded(0, chunk)
        for part in range(n_part):
            send_blocks(group, stage.at[group, chunk], chunk, part)

    ahead = min(2, n_chunk)
    for chunk in range(ahead):
        send_own(chunk)
        if chunk == 0:
            for step in range(n_group):
                send_weights(lax.rem(group + step, n_group))
    for chunk, part in pieces:
        for step in range(1, n_group):
            origin = lax.rem(group + step, n_group)
            if (chunk, part) in passed:
                block = relay.at[origin, chunk, pl.ds(part * size, size)]
                pltpu.make_async_copy(
                    block, block, relay_sem.at[origin, chunk, part]
                ).wait()
                send_blocks(origin, relay.at[origin, chunk], chunk, part)
            else:
                send_far(step, chunk, part)
        if part == n_part - 1 and chunk + ahead < n_chunk:
            send_own(chunk + ahead)

    points = grid_ref.shape[1]
    on_diagonal = lax.broadcasted_iota(jnp.int32, (points, points), 0) == lax.broadcasted_iota(
        jnp.int32, (points, points), 1
    )
    column = jnp.sum(jnp.where(on_diagonal, grid_ref[...], 0.0), axis=1, keepdims=True)
    grid_col[...] = jnp.broadcast_to(column, (points, LANES))

    pltpu.make_async_copy(weights, weights, wrecv_sem).wait()
    total = jnp.zeros((1, 1), jnp.float32)
    for c in range(n_cfg):
        total = total + jnp.sum(weights[c], axis=1, keepdims=True)
    for c in range(n_cfg):
        scaled = weights[c] / total
        for j in range(own):
            norm[c * own + j] = jnp.broadcast_to(scaled[:, j:j + 1], (1, LANES))

    shape = (tiles, LANES)
    for chunk in range(n_chunk):
        pltpu.make_async_copy(landed.at[chunk], landed.at[chunk], recv_sem.at[chunk]).wait()

        def value(c, a, j):
            return landed[chunk, c, a, pl.ds(j, tiles, stride=own), :]

        def add_mode(c, acc):
            for j in range(own):
                acc = acc + norm[c * own + j] * value(c, 0, j)
            return acc

        centre = over(n_cfg, add_mode, jnp.zeros(shape, jnp.float32))

        def add_var(c, acc):
            for j in range(own):
                off = value(c, 0, j) - centre
                acc = acc + norm[c * own + j] * (value(c, 1, j) + off * off)
            return acc

        spread = jnp.sqrt(over(n_cfg, add_var, jnp.zeros(shape, jnp.float32)))
        moments_ref[pl.ds(2 * tiles * chunk, tiles, stride=2), :] = centre
        moments_ref[pl.ds(2 * tiles * chunk + 1, tiles, stride=2), :] = spread

        def prepare(c, carry):
            for j in range(own):
                k = c * own + j
                root = lax.rsqrt(value(c, 1, j))
                scale = root * math.sqrt(HALF_LOG2E)
                rows_u[k] = spread * scale
                rows_v[k] = (centre - value(c, 0, j)) * scale
                rows_c[k] = jnp.log2(norm[k] * spread * root * (1.0 / math.sqrt(TWO_PI)))
            return carry

        over(n_cfg, prepare, 0)

        if chunk < n_chunk - 1:
            densities(
                grid_col, rows_u, rows_v, rows_c, density_ref, chunk * tiles
            )

    def spent(block, sem):
        pltpu.make_async_copy(block, block, sem).wait()

    for step in range(n_group):
        origin = lax.rem(group + step, n_group)

        def drain(i, carry):
            flat, _ = target(origin, i)

            @pl.when(flat != me)
            def _():
                spent(weight_ref, wsend_sem.at[origin, i])

            def drain_blocks(n):
                @pl.when(flat != me)
                def _():
                    spent(landed.at[pl.ds(0, n), 0], send_sem.at[origin, i])

            part = i // (CORES * size)
            if step == 0 or not n_far:
                drain_blocks(n_chunk)
            else:
                for p in range(n_part):
                    n = sum(1 for _, q in passed if q == p)
                    if n:
                        pl.when(part == p)(functools.partial(drain_blocks, n))
            return carry

        over(per_group, drain, 0)

        if step:
            for part in range(n_part):
                pieces_sent = [chunk for chunk, q in passed if q == part]
                span = pl.ds(part * size, size)
                if pieces_sent:
                    spent(stage.at[origin, pl.ds(0, len(pieces_sent)), span],
                          pass_sem.at[origin, part])
            for chunk, part in pieces[len(passed):]:
                def drain_far(i, carry):
                    spent(landed.at[0, 0], far_sem.at[origin, chunk, i])
                    return carry
                if size * CORES <= 16:
                    for i in range(size * CORES):
                        drain_far(i + part * size * CORES, 0)
                else:
                    lax.fori_loop(part * size * CORES, (part + 1) * size * CORES, drain_far, 0)


def finish(
    n_chunk, tiles,
    done_ref, made_ref, rows_u, rows_v, rows_c, grid_col,
    density_ref, moments_ref,
    last, sems,
):
    early = done_ref.shape[1]
    copies = [
        pltpu.make_async_copy(done_ref, density_ref.at[:, pl.ds(0, early)], sems.at[0]),
        pltpu.make_async_copy(made_ref, moments_ref, sems.at[1]),
    ]
    for copy in copies:
        copy.start()
    densities(grid_col, rows_u, rows_v, rows_c, last, 0)
    copies.append(
        pltpu.make_async_copy(
            last, density_ref.at[:, pl.ds(early, tiles * LANES)], sems.at[2]
        )
    )
    copies[2].start()
    for copy in copies:
        copy.wait()


def interleave(block, n_cfg, n_lat, n_chunk):
    own, columns = block.shape
    rows = block.reshape(own, columns // LANES, LANES).transpose(1, 0, 2)
    n_row = columns * own // (LANES * n_cfg * n_chunk)
    return rows.reshape(n_cfg // n_lat, n_lat // CORES, CORES, n_chunk, n_row, LANES)


def per_device(latent_mode, latent_var, config_weight, grid_offset):
    n_cfg = lax.axis_size("cfg")
    n_lat = lax.axis_size("lat")
    own, columns = latent_mode.shape
    lat_dev = columns // n_cfg
    points = grid_offset.shape[0]
    n_chunk = 4
    n_far = FAR
    tiles = lat_dev // (LANES * n_chunk)
    n_config = own * n_cfg
    n_group = n_lat // CORES
    per_group = n_cfg // n_group
    passing = (n_group, n_chunk, n_cfg // n_lat, CORES, 2, own * tiles, LANES)
    f32 = jnp.float32
    hbm = pl.BlockSpec(memory_space=pl.ANY)
    vmem = pl.BlockSpec(memory_space=pltpu.VMEM)
    early = lat_dev - tiles * LANES
    interleaved = (2 * lat_dev // LANES, LANES)
    rows = (n_config, tiles, LANES)
    parts = pl.pallas_call(
        functools.partial(kernel, n_cfg, n_lat, own, n_chunk, n_far, tiles),
        out_shape=(
            pltpu.VMEM((points, early), f32),
            pltpu.VMEM(interleaved, f32),
            pltpu.VMEM(rows, f32),
            pltpu.VMEM(rows, f32),
            pltpu.VMEM(rows, f32),
            pltpu.VMEM((points, LANES), f32),
        ),
        in_specs=[hbm, hbm, vmem, vmem],
        out_specs=(vmem,) * 6,
        scratch_shapes=[
            pltpu.VMEM(passing, f32),
            pltpu.VMEM(passing, f32),
            pltpu.VMEM((n_chunk, n_cfg, 2, own * tiles, LANES), f32),
            pltpu.VMEM((n_cfg, 1, own), f32),
            pltpu.VMEM((n_config, 1, LANES), f32),
            pltpu.SemaphoreType.DMA((n_group, n_chunk)),
            pltpu.SemaphoreType.DMA((n_group, 2)),
            pltpu.SemaphoreType.DMA((n_group, n_chunk, 2)),
            pltpu.SemaphoreType.DMA((n_group, n_chunk, per_group)),
            pltpu.SemaphoreType.DMA((n_group, per_group)),
            pltpu.SemaphoreType.DMA((n_chunk,)),
            pltpu.SemaphoreType.DMA((n_group, per_group)),
            pltpu.SemaphoreType.DMA,
        ],
        compiler_params=pltpu.CompilerParams(collective_id=0, has_side_effects=True),
    )(
        interleave(latent_mode, n_cfg, n_lat, n_chunk),
        interleave(latent_var, n_cfg, n_lat, n_chunk),
        config_weight.reshape(1, own),
        grid_offset.reshape(1, points),
    )
    density, moments = pl.pallas_call(
        functools.partial(finish, n_chunk, tiles),
        out_shape=(
            jax.ShapeDtypeStruct((points, lat_dev), f32),
            jax.ShapeDtypeStruct(interleaved, f32),
        ),
        in_specs=[vmem] * 6,
        out_specs=(hbm, hbm),
        scratch_shapes=[
            pltpu.VMEM((points, tiles * LANES), f32),
            pltpu.SemaphoreType.DMA((3,)),
        ],
    )(*(pltpu.with_memory_space_constraint(part, pltpu.VMEM) for part in parts))
    moments = moments.reshape(lat_dev // LANES, 2, LANES).transpose(1, 0, 2).reshape(2, lat_dev)
    return (density, moments)


def solution(mesh):
    return jax.shard_map(
        per_device,
        mesh=mesh,
        in_specs=(P("cfg", "lat"), P("cfg", "lat"), P("cfg"), P()),
        out_specs=(P(None, ("cfg", "lat")), P(None, ("cfg", "lat"))),
        check_vma=False,
    )
```

profile of v0, /device:TPU:3, one launch (start us, length us, event | category | flops | bytes accessed | tf_op | source)
XLA Modules:
  0.0 22.7 jit_solution(2340727912294501086)
XLA Ops:
  0.6 20.4 %shard_map.59 = (f32[64,3072]{1,0:T(8,128)S(1)}, f32[64,128]{1,0:T(8,128)S(1)}, f32[16,8,128]{2,1,0:T(8,128)S(1)}, f32[16,8,128]{2,1,0:T(8,128)S(1)}, f32[16,8,128]{2,1,0:T(8,128)S(1)}, /*index=5*/f32[64,128]{1,0:T(8,128)S(1)}) custom-call(f32[2,2,2,4,16,128]{5,4,3,2,1,0:T(8,128)} %bitcast.17, f32[2,2,2,4,16,128]{5,4,3,2,1,0:T(8,128)} %bitcast.18, ...), custom_call_target="tpu_custom_call" | custom-call | tf_op jit(solution)/shard_map/pallas_call | solution.py:372
  21.0 1.6 %shard_map.60 = (f32[64,4096]{1,0:T(8,128)}, f32[64,128]{1,0:T(8,128)}) custom-call(f32[64,3072]{1,0:T(8,128)S(1)} %get-tuple-element.10.done_ref, f32[64,128]{1,0:T(8,128)S(1)} %get-tuple-element.11.made_ref, f32[16,8,128]{2,1,0:T(8,128)S(1)} %get-tuple-element.12.rows_u, f32[16,8,128]{2,1,0:T(8,128)S(1)} %get-tuple-element.13.rows_v, ...), custom_call_target="tpu_custom_call" | custom-call | tf_op jit(solution)/shard_map/pallas_call | solution.py:406
where the time goes:
time: 23 us; the launch traced here: 22.7 us
  Pallas kernels  22 us (96%)
  between operations  0.64 us (3%)
    pallas_call x1, Pallas kernels, per_device(): pl.pallas_call(functools.partial(kernel, n_cfg, n_lat, own, n_chunk, n_fa...  20.4 us
    pallas_call x1, Pallas kernels, per_device(): pl.pallas_call(functools.partial(finish, n_chunk, tiles), out_shape=(jax....  1.64 us

commit v1 on v0

--- a/solution.py
+++ b/solution.py
@@ -11,6 +11,7 @@
 LANES = 128
 CORES = 2
 FAR = 0
+AHEAD = 2
 MESH = pl.DeviceIdType.MESH
 HALF_LOG2E = 0.5 * math.log2(math.e)
 TWO_PI = 6.283185307179586
@@ -43,10 +44,10 @@
 
 def kernel(
     n_cfg, n_lat, own, n_chunk, n_far, tiles,
-    mode_ref, var_ref, weight_ref, grid_ref,
+    mode_ref, var_ref, weight_hbm, grid_hbm,
     density_ref, moments_ref, rows_u, rows_v, rows_c, grid_col,
-    stage, relay, landed, weights, norm,
-    load_sem, pass_sem, relay_sem, far_sem, send_sem, recv_sem, wsend_sem, wrecv_sem,
+    stage, relay, landed, weights, norm, weight_ref, grid_ref,
+    small_sem, go_sem, load_sem, pass_sem, relay_sem, far_sem, send_sem, recv_sem, wsend_sem, wrecv_sem,
 ):
     my_cfg = lax.axis_index("cfg")
     my_lat = lax.axis_index("lat")
@@ -56,50 +57,54 @@
     n_config = n_cfg * own
     per_group = n_cfg // n_group
 
+    def load(step, chunk):
+        to = lax.rem(group + step, n_group)
+        for a, ref in enumerate((mode_ref, var_ref)):
+            pltpu.make_async_copy(
+                ref.at[:, to, :, chunk], stage.at[to, chunk, :, :, a],
+                load_sem.at[step, chunk],
+            ).start()
+
     barrier = pltpu.get_barrier_semaphore()
-    sender = group * CORES + lax.rem(me // n_cfg, CORES)
-
-    def greet(i, carry):
-        @pl.when(jnp.logical_or(i != my_cfg, sender != my_lat))
-        def _():
-            pl.semaphore_signal(
-                barrier, inc=1, device_id=(i, sender), device_id_type=MESH
-            )
-        return carry
+    gate = CORES - 1
 
     for step in range(1, n_group):
         peer = lax.rem(group + step, n_group) * CORES + core
         pl.semaphore_signal(
             barrier, inc=1, device_id=(my_cfg, peer), device_id_type=MESH
         )
+
+    def greet(i, carry):
+        @pl.when(jnp.logical_or(i != my_cfg, core != gate))
+        def _():
+            pl.semaphore_signal(
+                barrier, inc=1, device_id=(i, group * CORES + gate), device_id_type=MESH
+            )
+        return carry
+
     over(n_cfg, greet, 0)
-    waits = n_group - 1 + n_cfg
-    if n_far:
-        waits = waits + n_cfg - per_group
-        origin_lat = me // n_cfg
-
-        def greet_far(i, carry):
-            @pl.when(origin_lat // CORES != group)
-            def _():
-                pl.semaphore_signal(
-                    barrier, inc=1, device_id=(i, origin_lat), device_id_type=MESH
-                )
-            return carry
-
-        over(n_cfg, greet_far, 0)
-
 
     for chunk in range(n_chunk):
-        for step in list(range(1, n_group)) + [0]:
-            to = lax.rem(group + step, n_group)
-            for a, ref in enumerate((mode_ref, var_ref)):
-                pltpu.make_async_copy(
-                    ref.at[:, to, :, chunk], stage.at[to, chunk, :, :, a],
-                    load_sem.at[step, chunk],
-                ).start()
-
-    keeps = (sender == my_lat).astype(jnp.int32)
-    pl.semaphore_wait(barrier, waits - keeps)
+        for step in range(1, n_group):
+            load(step, chunk)
+    for chunk in range(n_chunk):
+        load(0, chunk)
+    small = [
+        pltpu.make_async_copy(weight_hbm, weight_ref, small_sem.at[0]),
+        pltpu.make_async_copy(grid_hbm, grid_ref, small_sem.at[1]),
+    ]
+    for copy in small:
+        copy.start()
+
+    everyone = n_group - 1 + n_cfg * CORES - 1
+    pl.semaphore_wait(barrier, jnp.where(core == gate, everyone, n_group - 1))
+
+    @pl.when(core == gate)
+    def _():
+        for other in range(CORES - 1):
+            pl.semaphore_signal(
+                go_sem, inc=1, device_id=(my_cfg, group * CORES + other), device_id_type=MESH
+            )
 
     def loaded(step, chunk):
         to = lax.rem(group + step, n_group)
@@ -194,7 +199,12 @@
         for part in range(n_part):
             send_blocks(group, stage.at[group, chunk], chunk, part)
 
-    ahead = min(2, n_chunk)
+    @pl.when(core != gate)
+    def _():
+        pl.semaphore_wait(go_sem, 1)
+
+    small[0].wait()
+    ahead = min(AHEAD, n_chunk)
     for chunk in range(ahead):
         send_own(chunk)
         if chunk == 0:
@@ -214,6 +224,7 @@
         if part == n_part - 1 and chunk + ahead < n_chunk:
             send_own(chunk + ahead)
 
+    small[1].wait()
     points = grid_ref.shape[1]
     on_diagonal = lax.broadcasted_iota(jnp.int32, (points, points), 0) == lax.broadcasted_iota(
         jnp.int32, (points, points), 1
@@ -230,8 +241,58 @@
         for j in range(own):
             norm[c * own + j] = jnp.broadcast_to(scaled[:, j:j + 1], (1, LANES))
 
+    def drain_all():
+        def spent(block, sem):
+            pltpu.make_async_copy(block, block, sem).wait()
+
+        for step in range(n_group):
+            origin = lax.rem(group + step, n_group)
+
+            def drain(i, carry):
+                flat, _ = target(origin, i)
+
+                @pl.when(flat != me)
+                def _():
+                    spent(weight_ref, wsend_sem.at[origin, i])
+
+                def drain_blocks(n):
+                    @pl.when(flat != me)
+                    def _():
+                        spent(landed.at[pl.ds(0, n), 0], send_sem.at[origin, i])
+
+                part = i // (CORES * size)
+                if step == 0 or not n_far:
+                    drain_blocks(n_chunk)
+                else:
+                    for p in range(n_part):
+                        n = sum(1 for _, q in passed if q == p)
+                        if n:
+                            pl.when(part == p)(functools.partial(drain_blocks, n))
+                return carry
+
+            over(per_group, drain, 0)
+
+            if step:
+                for part in range(n_part):
+                    pieces_sent = [chunk for chunk, q in passed if q == part]
+                    span = pl.ds(part * size, size)
+                    if pieces_sent:
+                        spent(stage.at[origin, pl.ds(0, len(pieces_sent)), span],
+                              pass_sem.at[origin, part])
+                for chunk, part in pieces[len(passed):]:
+                    def drain_far(i, carry):
+                        spent(landed.at[0, 0], far_sem.at[origin, chunk, i])
+                        return carry
+                    if size * CORES <= 16:
+                        for i in range(size * CORES):
+                            drain_far(i + part * size * CORES, 0)
+                    else:
+                        lax.fori_loop(part * size * CORES, (part + 1) * size * CORES, drain_far, 0)
+
     shape = (tiles, LANES)
     for chunk in range(n_chunk):
+        if chunk == n_chunk - 1:
+            drain_all()
         pltpu.make_async_copy(landed.at[chunk], landed.at[chunk], recv_sem.at[chunk]).wait()
 
         def value(c, a, j):
@@ -270,53 +331,6 @@
             densities(
                 grid_col, rows_u, rows_v, rows_c, density_ref, chunk * tiles
             )
-
-    def spent(block, sem):
-        pltpu.make_async_copy(block, block, sem).wait()
-
-    for step in range(n_group):
-        origin = lax.rem(group + step, n_group)
-
-        def drain(i, carry):
-            flat, _ = target(origin, i)
-
-            @pl.when(flat != me)
-            def _():
-                spent(weight_ref, wsend_sem.at[origin, i])
-
-            def drain_blocks(n):
-                @pl.when(flat != me)
-                def _():
-                    spent(landed.at[pl.ds(0, n), 0], send_sem.at[origin, i])
-
-            part = i // (CORES * size)
-            if step == 0 or not n_far:
-                drain_blocks(n_chunk)
-            else:
-                for p in range(n_part):
-                    n = sum(1 for _, q in passed if q == p)
-                    if n:
-                        pl.when(part == p)(functools.partial(drain_blocks, n))
-            return carry
-
-        over(per_group, drain, 0)
-
-        if step:
-            for part in range(n_part):
-                pieces_sent = [chunk for chunk, q in passed if q == part]
-                span = pl.ds(part * size, size)
-                if pieces_sent:
-                    spent(stage.at[origin, pl.ds(0, len(pieces_sent)), span],
-                          pass_sem.at[origin, part])
-            for chunk, part in pieces[len(passed):]:
-                def drain_far(i, carry):
-                    spent(landed.at[0, 0], far_sem.at[origin, chunk, i])
-                    return carry
-                if size * CORES <= 16:
-                    for i in range(size * CORES):
-                        drain_far(i + part * size * CORES, 0)
-                else:
-                    lax.fori_loop(part * size * CORES, (part + 1) * size * CORES, drain_far, 0)
 
 
 def finish(
@@ -379,7 +393,7 @@
             pltpu.VMEM(rows, f32),
             pltpu.VMEM((points, LANES), f32),
         ),
-        in_specs=[hbm, hbm, vmem, vmem],
+        in_specs=[hbm, hbm, hbm, hbm],
         out_specs=(vmem,) * 6,
         scratch_shapes=[
             pltpu.VMEM(passing, f32),
@@ -387,6 +401,10 @@
             pltpu.VMEM((n_chunk, n_cfg, 2, own * tiles, LANES), f32),
             pltpu.VMEM((n_cfg, 1, own), f32),
             pltpu.VMEM((n_config, 1, LANES), f32),
+            pltpu.VMEM((1, own), f32),
+            pltpu.VMEM((1, points), f32),
+            pltpu.SemaphoreType.DMA((2,)),
+            pltpu.SemaphoreType.REGULAR,
             pltpu.SemaphoreType.DMA((n_group, n_chunk)),
             pltpu.SemaphoreType.DMA((n_group, 2)),
             pltpu.SemaphoreType.DMA((n_group, n_chunk, 2)),

time: 23 us -> 22.3 us (0.970)
  Pallas kernels: 22 us -> 21.4 us
    pallas_call x1, Pallas kernels: 20.4 us -> 19.8 us  [per_device(): pl.pallas_call(functools.partial(kernel, n_cfg, n_lat, own, n_chunk, n_fa...]
where the time goes in v1:
time: 22.3 us; the launch traced here: 22 us
  Pallas kernels  21.4 us (96%)
  between operations  0.64 us (3%)
    pallas_call x1, Pallas kernels, per_device(): pl.pallas_call(functools.partial(kernel, n_cfg, n_lat, own, n_chunk, n_fa...  19.8 us
    pallas_call x1, Pallas kernels, per_device(): pl.pallas_call(functools.partial(finish, n_chunk, tiles), out_shape=(jax....  1.64 us

profile of v1, /device:TPU:3, one launch (start us, length us, event | category | flops | bytes accessed | tf_op | source)
XLA Modules:
  0.0 22.0 jit_solution(15829358924810286777)
XLA Ops:
  0.6 19.8 %shard_map.59 = (f32[64,3072]{1,0:T(8,128)S(1)}, f32[64,128]{1,0:T(8,128)S(1)}, f32[16,8,128]{2,1,0:T(8,128)S(1)}, f32[16,8,128]{2,1,0:T(8,128)S(1)}, f32[16,8,128]{2,1,0:T(8,128)S(1)}, /*index=5*/f32[64,128]{1,0:T(8,128)S(1)}) custom-call(f32[2,2,2,4,16,128]{5,4,3,2,1,0:T(8,128)} %bitcast.17, f32[2,2,2,4,16,128]{5,4,3,2,1,0:T(8,128)} %bitcast.18, ...), custom_call_target="tpu_custom_call" | custom-call | tf_op jit(solution)/shard_map/pallas_call | solution.py:386
  20.4 1.6 %shard_map.60 = (f32[64,4096]{1,0:T(8,128)}, f32[64,128]{1,0:T(8,128)}) custom-call(f32[64,3072]{1,0:T(8,128)S(1)} %get-tuple-element.10.done_ref, f32[64,128]{1,0:T(8,128)S(1)} %get-tuple-element.11.made_ref, f32[16,8,128]{2,1,0:T(8,128)S(1)} %get-tuple-element.12.rows_u, f32[16,8,128]{2,1,0:T(8,128)S(1)} %get-tuple-element.13.rows_v, ...), custom_call_target="tpu_custom_call" | custom-call | tf_op jit(solution)/shard_map/pallas_call | solution.py:424

commit v2 on v1

v2 whole, which is shorter than its diff:
```python
import functools
import math

import jax
import jax.numpy as jnp
from jax import lax
from jax.experimental import pallas as pl
from jax.experimental.pallas import tpu as pltpu
from jax.sharding import PartitionSpec as P

LANES = 128
CORES = 2
UNITS = (2, 2, 2, 1, 1)
AHEAD = 2
HOPS = 5
MESH = pl.DeviceIdType.MESH
HALF_LOG2E = 0.5 * math.log2(math.e)
TWO_PI = 6.283185307179586


def over(n, body, init):
    if n <= 16:
        for i in range(n):
            init = body(i, init)
        return init
    return lax.fori_loop(0, n, body, init)


def densities(grid_col, rows_u, rows_v, rows_c, tiles, out_ref, first):
    n_config = rows_u.shape[0]
    grid = grid_col[...]

    def one_tile(t, carry):
        def term(k, acc):
            at = grid * rows_u[k, pl.ds(t, 1), :] + rows_v[k, pl.ds(t, 1), :]
            return acc + jnp.exp2(rows_c[k, pl.ds(t, 1), :] - at * at)

        acc = over(n_config, term, jnp.zeros(grid.shape, jnp.float32))
        column_at = pl.multiple_of((first + t) * LANES, LANES)
        out_ref[:, pl.ds(column_at, LANES)] = acc
        return carry

    lax.fori_loop(0, tiles, one_tile, 0)


def kernel(
    n_cfg, n_lat, own, spans,
    mode_ref, var_ref, weight_hbm, grid_hbm,
    density_ref, moments_ref, last_u, last_v, last_c, grid_col,
    stage, relay, landed, weights, norm, weight_ref, grid_ref, rows_u, rows_v, rows_c,
    small_sem, go_sem, rest_sem, load_sem, pass_sem, relay_sem, send_sem, recv_sem, wsend_sem, wrecv_sem,
):
    my_cfg = lax.axis_index("cfg")
    my_lat = lax.axis_index("lat")
    me = my_cfg * n_lat + my_lat
    n_group = n_lat // CORES
    group, core = my_lat // CORES, lax.rem(my_lat, CORES)
    per_group = n_cfg // n_group
    n_chunk = len(spans)

    def rows_of(chunk, until=None):
        start = 2 * own * spans[chunk][0]
        t, n = spans[chunk if until is None else until]
        return pl.ds(start, 2 * own * (t + n) - start)

    barrier = pltpu.get_barrier_semaphore()
    half_cfg = n_cfg // 2
    half = my_cfg // half_cfg
    gate = 1 - half
    is_gate = core == gate

    for step in range(1, n_group):
        peer = lax.rem(group + step, n_group) * CORES + core
        pl.semaphore_signal(
            barrier, inc=1, device_id=(my_cfg, peer), device_id_type=MESH
        )

    def greet(i, carry):
        early = i < half_cfg
        mate = jnp.logical_and(i == my_cfg, core != gate)
        others = jnp.logical_and(i != my_cfg, jnp.logical_or(early, half == 0))

        @pl.when(jnp.logical_or(mate, others))
        def _():
            pl.semaphore_signal(
                barrier, inc=1,
                device_id=(i, group * CORES + jnp.where(early, 1, 0)), device_id_type=MESH,
            )
        return carry

    over(n_cfg, greet, 0)

    for chunk in range(n_chunk):
        start, tiles = spans[chunk]
        n_row = own * tiles
        for step in list(range(1, n_group)) + [0]:
            to = lax.rem(group + step, n_group)
            for a, ref in enumerate((mode_ref, var_ref)):
                pltpu.make_async_copy(
                    ref.at[:, to, :, pl.ds(own * start, n_row)],
                    stage.at[to, :, :, pl.ds(2 * own * start + a * n_row, n_row)],
                    load_sem.at[step, min(chunk, 1)],
                ).start()
    small = [
        pltpu.make_async_copy(weight_hbm, weight_ref, small_sem.at[0]),
        pltpu.make_async_copy(grid_hbm, grid_ref, small_sem.at[1]),
    ]
    for copy in small:
        copy.start()

    peers = n_group - 1
    gathered = jnp.where(half == 0, n_cfg * CORES - 1, half_cfg * CORES + 1)
    pl.semaphore_wait(barrier, peers + jnp.where(is_gate, gathered, 0))

    @pl.when(is_gate)
    def _():
        pl.semaphore_signal(
            go_sem, inc=1, device_id=(my_cfg, group * CORES + 1 - gate), device_id_type=MESH
        )

        @pl.when(half == 0)
        def _():
            for other in range(CORES):
                pl.semaphore_signal(
                    rest_sem, inc=1,
                    device_id=(my_cfg + half_cfg, group * CORES + other), device_id_type=MESH,
                )

    def spent(block, sem):
        pltpu.make_async_copy(block, block, sem).wait()

    def loaded(step, chunk):
        to = lax.rem(group + step, n_group)
        if chunk == 0:
            spent(stage.at[to, :, :, rows_of(0)], load_sem.at[step, 0])
        if chunk == 1:
            spent(stage.at[to, :, :, rows_of(1, n_chunk - 1)], load_sem.at[step, 1])

    def hop(chunk):
        for step in range(1, n_group):
            to = lax.rem(group + step, n_group)
            loaded(step, chunk)
            slot = n_group - step - 1
            pltpu.make_async_remote_copy(
                src_ref=stage.at[to, :, :, rows_of(chunk)],
                dst_ref=relay.at[slot, :, :, rows_of(chunk)],
                send_sem=pass_sem, recv_sem=relay_sem.at[slot, chunk],
                device_id=(my_cfg, to * CORES + core), device_id_type=MESH,
            ).start()

    hops = min(HOPS, n_chunk)
    for chunk in range(hops):
        hop(chunk)

    @pl.when(jnp.logical_not(is_gate))
    def _():
        pl.semaphore_wait(go_sem, 1)

    for chunk in range(hops, n_chunk):
        hop(chunk)

    def target(origin, i):
        slot = (i // CORES) * n_lat + group * CORES + i % CORES
        flat = (origin * CORES + core) * n_cfg + slot
        return flat, (flat // n_lat, lax.rem(flat, n_lat))

    def send_weights(origin):
        def send(i, carry):
            flat, device = target(origin, i)

            @pl.when(flat == me)
            def _():
                pltpu.make_async_copy(weight_ref, weights.at[my_cfg], wrecv_sem).start()

            @pl.when(flat != me)
            def _():
                pltpu.make_async_remote_copy(
                    src_ref=weight_ref, dst_ref=weights.at[my_cfg],
                    send_sem=wsend_sem, recv_sem=wrecv_sem,
                    device_id=device, device_id_type=MESH,
                ).start()
            return carry

        over(per_group, send, 0)

    def send_blocks(origin, source, chunk):
        rows = rows_of(chunk)

        def send(i, carry):
            flat, device = target(origin, i)
            src = source.at[i // CORES, i % CORES, rows]
            dst = landed.at[my_cfg, rows]

            @pl.when(flat == me)
            def _():
                pltpu.make_async_copy(src, dst, recv_sem.at[chunk]).start()

            @pl.when(flat != me)
            def _():
                pltpu.make_async_remote_copy(
                    src_ref=src, dst_ref=dst,
                    send_sem=send_sem, recv_sem=recv_sem.at[chunk],
                    device_id=device, device_id_type=MESH,
                ).start()
            return carry

        over(per_group, send, 0)

    def send_own(chunk):
        loaded(0, chunk)
        send_blocks(group, stage.at[group], chunk)

    def crosses(origin):
        return (origin * CORES + core) * 2 // n_lat != half

    def send_relayed(chunk):
        for step in range(1, n_group):
            origin = lax.rem(group + step, n_group)
            block = relay.at[step - 1, :, :, rows_of(chunk)]
            spent(block, relay_sem.at[step - 1, chunk])
            send_blocks(origin, relay.at[step - 1], chunk)

    own_first = crosses(group)

    def weights_where(first):
        for origin in range(n_group):
            @pl.when(crosses(origin) == first)
            def _():
                send_weights(origin)

    small[0].wait()
    weights_where(True)

    @pl.when(half == 0)
    def _():
        weights_where(False)

    @pl.when(jnp.logical_or(half == 0, own_first))
    def _():
        for chunk in range(n_chunk):
            send_own(chunk)

    ahead = min(AHEAD, n_chunk)

    @pl.when(jnp.logical_not(own_first))
    def _():
        for chunk in range(ahead):
            send_relayed(chunk)

    @pl.when(half == 1)
    def _():
        pl.semaphore_wait(rest_sem, 1)
        weights_where(False)

        @pl.when(jnp.logical_not(own_first))
        def _():
            for chunk in range(n_chunk):
                send_own(chunk)

    @pl.when(own_first)
    def _():
        for chunk in range(ahead):
            send_relayed(chunk)

    for chunk in range(ahead, n_chunk):
        send_relayed(chunk)

    small[1].wait()
    points = grid_ref.shape[1]
    on_diagonal = lax.broadcasted_iota(jnp.int32, (points, points), 0) == lax.broadcasted_iota(
        jnp.int32, (points, points), 1
    )
    column = jnp.sum(jnp.where(on_diagonal, grid_ref[...], 0.0), axis=1, keepdims=True)
    grid_col[...] = jnp.broadcast_to(column, (points, LANES))

    pltpu.make_async_copy(weights, weights, wrecv_sem).wait()
    total = jnp.zeros((1, 1), jnp.float32)
    for c in range(n_cfg):
        total = total + jnp.sum(weights[c], axis=1, keepdims=True)
    for c in range(n_cfg):
        scaled = weights[c] / total
        for j in range(own):
            norm[c * own + j] = jnp.broadcast_to(scaled[:, j:j + 1], (1, LANES))

    for chunk in range(n_chunk):
        start, tiles = spans[chunk]
        base = 2 * own * start
        n_row = own * tiles
        shape = (tiles, LANES)
        arrived = landed.at[:, rows_of(chunk)]
        pltpu.make_async_copy(arrived, arrived, recv_sem.at[chunk]).wait()

        def value(c, a, j):
            return landed[c, pl.ds(base + a * n_row + j, tiles, stride=own), :]

        def add_mode(c, acc):
            for j in range(own):
                acc = acc + norm[c * own + j] * value(c, 0, j)
            return acc

        centre = over(n_cfg, add_mode, jnp.zeros(shape, jnp.float32))

        def add_var(c, acc):
            for j in range(own):
                off = value(c, 0, j) - centre
                acc = acc + norm[c * own + j] * (value(c, 1, j) + off * off)
            return acc

        spread = jnp.sqrt(over(n_cfg, add_var, jnp.zeros(shape, jnp.float32)))
        moments_ref[pl.ds(2 * start, tiles, stride=2), :] = centre
        moments_ref[pl.ds(2 * start + 1, tiles, stride=2), :] = spread

        final = chunk == n_chunk - 1
        to_u, to_v, to_c = (last_u, last_v, last_c) if final else (rows_u, rows_v, rows_c)

        def prepare(c, carry):
            for j in range(own):
                k = c * own + j
                root = lax.rsqrt(value(c, 1, j))
                scale = root * math.sqrt(HALF_LOG2E)
                to_u[k, pl.ds(0, tiles)] = spread * scale
                to_v[k, pl.ds(0, tiles)] = (centre - value(c, 0, j)) * scale
                to_c[k, pl.ds(0, tiles)] = jnp.log2(
                    norm[k] * spread * root * (1.0 / math.sqrt(TWO_PI))
                )
            return carry

        over(n_cfg, prepare, 0)

        if not final:
            densities(
                grid_col, rows_u, rows_v, rows_c, tiles, density_ref, start
            )

    spent(stage.at[pl.ds(0, n_group - 1)], pass_sem)
    for kept, n in ((lax.rem(me // n_cfg, CORES) == core, n_cfg - 1),
                    (lax.rem(me // n_cfg, CORES) != core, n_cfg)):
        @pl.when(kept)
        def _():
            spent(weights.at[pl.ds(0, n)], wsend_sem)
            spent(landed.at[pl.ds(0, n)], send_sem)


def finish(
    tiles,
    done_ref, made_ref, rows_u, rows_v, rows_c, grid_col,
    density_ref, moments_ref,
    last, sems,
):
    early = done_ref.shape[1]
    copies = [
        pltpu.make_async_copy(done_ref, density_ref.at[:, pl.ds(0, early)], sems.at[0]),
        pltpu.make_async_copy(made_ref, moments_ref, sems.at[1]),
    ]
    for copy in copies:
        copy.start()
    densities(grid_col, rows_u, rows_v, rows_c, tiles, last, 0)
    copies.append(
        pltpu.make_async_copy(
            last, density_ref.at[:, pl.ds(early, tiles * LANES)], sems.at[2]
        )
    )
    copies[2].start()
    for copy in copies:
        copy.wait()


def interleave(block, n_cfg, n_lat):
    own, columns = block.shape
    rows = block.reshape(own, columns // LANES, LANES).transpose(1, 0, 2)
    n_row = columns * own // (LANES * n_cfg)
    return rows.reshape(n_cfg // n_lat, n_lat // CORES, CORES, n_row, LANES)


def per_device(latent_mode, latent_var, config_weight, grid_offset):
    n_cfg = lax.axis_size("cfg")
    n_lat = lax.axis_size("lat")
    own, columns = latent_mode.shape
    lat_dev = columns // n_cfg
    points = grid_offset.shape[0]
    unit = lat_dev // (LANES * sum(UNITS))
    spans = []
    for n in UNITS:
        spans.append((sum(s[1] for s in spans), n * unit))
    most, last = max(n for _, n in spans[:-1]), spans[-1][1]
    n_chunk = len(spans)
    n_config = own * n_cfg
    n_group = n_lat // CORES
    n_row = 2 * own * lat_dev // LANES
    n_a = n_cfg // n_lat
    f32 = jnp.float32
    hbm = pl.BlockSpec(memory_space=pl.ANY)
    vmem = pl.BlockSpec(memory_space=pltpu.VMEM)
    early = lat_dev - last * LANES
    interleaved = (2 * lat_dev // LANES, LANES)
    dma = pltpu.SemaphoreType.DMA
    parts = pl.pallas_call(
        functools.partial(kernel, n_cfg, n_lat, own, spans),
        out_shape=(
            pltpu.VMEM((points, early), f32),
            pltpu.VMEM(interleaved, f32),
            pltpu.VMEM((n_config, last, LANES), f32),
            pltpu.VMEM((n_config, last, LANES), f32),
            pltpu.VMEM((n_config, last, LANES), f32),
            pltpu.VMEM((points, LANES), f32),
        ),
        in_specs=[hbm] * 4,
        out_specs=(vmem,) * 6,
        scratch_shapes=[
            pltpu.VMEM((n_group, n_a, CORES, n_row, LANES), f32),
            pltpu.VMEM((n_group - 1, n_a, CORES, n_row, LANES), f32),
            pltpu.VMEM((n_cfg, n_row, LANES), f32),
            pltpu.VMEM((n_cfg, 1, own), f32),
            pltpu.VMEM((n_config, 1, LANES), f32),
            pltpu.VMEM((1, own), f32),
            pltpu.VMEM((1, points), f32),
            pltpu.VMEM((n_config, most, LANES), f32),
            pltpu.VMEM((n_config, most, LANES), f32),
            pltpu.VMEM((n_config, most, LANES), f32),
            dma((2,)),
            pltpu.SemaphoreType.REGULAR,
            pltpu.SemaphoreType.REGULAR,
            dma((n_group, 2)),
            dma,
            dma((n_group - 1, n_chunk)),
            dma,
            dma((n_chunk,)),
            dma,
            dma,
        ],
        compiler_params=pltpu.CompilerParams(collective_id=0, has_side_effects=True),
    )(
        interleave(latent_mode, n_cfg, n_lat),
        interleave(latent_var, n_cfg, n_lat),
        config_weight.reshape(1, own),
        grid_offset.reshape(1, points),
    )
    density, moments = pl.pallas_call(
        functools.partial(finish, last),
        out_shape=(
            jax.ShapeDtypeStruct((points, lat_dev), f32),
            jax.ShapeDtypeStruct(interleaved, f32),
        ),
        in_specs=[vmem] * 6,
        out_specs=(hbm, hbm),
        scratch_shapes=[
            pltpu.VMEM((points, last * LANES), f32),
            dma((3,)),
        ],
    )(*(pltpu.with_memory_space_constraint(part, pltpu.VMEM) for part in parts))
    moments = moments.reshape(lat_dev // LANES, 2, LANES).transpose(1, 0, 2).reshape(2, lat_dev)
    return (density, moments)


def solution(mesh):
    return jax.shard_map(
        per_device,
        mesh=mesh,
        in_specs=(P("cfg", "lat"), P("cfg", "lat"), P("cfg"), P()),
        out_specs=(P(None, ("cfg", "lat")), P(None, ("cfg", "lat"))),
        check_vma=False,
    )
```

time: 22.3 us -> 21.3 us (0.955)
  Pallas kernels: 21.4 us -> 20.5 us
    pallas_call x2, Pallas kernels: 21.4 us -> 20.5 us  [the longest x1 19.4 us: per_device(): pl.pallas_call(functools.partial(kernel, n_cfg, n_lat, own, spans), out_s...]
where the time goes in v2:
time: 21.3 us; the launch traced here: 21.2 us
  Pallas kernels  20.5 us (96%)
  between operations  0.64 us (3%)
    pallas_call x1, Pallas kernels, per_device(): pl.pallas_call(functools.partial(kernel, n_cfg, n_lat, own, spans), out_s...  19.4 us
    pallas_call x1, Pallas kernels, per_device(): pl.pallas_call(functools.partial(finish, last), out_shape=(jax.ShapeDtype...  1.14 us

profile of v2, /device:TPU:3, one launch (start us, length us, event | category | flops | bytes accessed | tf_op | source)
XLA Modules:
  0.0 21.2 jit_solution(10552896517955903909)
XLA Ops:
  0.6 19.4 %shard_map.59 = (f32[64,3584]{1,0:T(8,128)S(1)}, f32[64,128]{1,0:T(8,128)S(1)}, f32[16,4,128]{2,1,0:T(4,128)S(1)}, f32[16,4,128]{2,1,0:T(4,128)S(1)}, f32[16,4,128]{2,1,0:T(4,128)S(1)}, /*index=5*/f32[64,128]{1,0:T(8,128)S(1)}) custom-call(f32[2,2,2,64,128]{4,3,2,1,0:T(8,128)} %bitcast.17, f32[2,2,2,64,128]{4,3,2,1,0:T(8,128)} %bitcast.18, f32[1,2]{1,0:T(1,128)} %bitcast.19, ...), custom_call_target="tpu_custom_call" | custom-call | tf_op jit(solution)/shard_map/pallas_call | solution.py:397
  20.0 1.1 %shard_map.60 = (f32[64,4096]{1,0:T(8,128)}, f32[64,128]{1,0:T(8,128)}) custom-call(f32[64,3584]{1,0:T(8,128)S(1)} %get-tuple-element.10.done_ref, f32[64,128]{1,0:T(8,128)S(1)} %get-tuple-element.11.made_ref, f32[16,4,128]{2,1,0:T(4,128)S(1)} %get-tuple-element.12.rows_u, f32[16,4,128]{2,1,0:T(4,128)S(1)} %get-tuple-element.13.rows_v, ...), custom_call_target="tpu_custom_call" | custom-call | tf_op jit(solution)/shard_map/pallas_call | solution.py:438

commit v3 on v2

--- a/solution.py
+++ b/solution.py
@@ -10,9 +10,10 @@
 
 LANES = 128
 CORES = 2
-UNITS = (2, 2, 2, 1, 1)
-AHEAD = 2
-HOPS = 5
+UNITS = (1, 1, 1, 1, 1, 1, 1, 1)
+AHEAD = 4
+LEAD = 4
+HOLD = (8, 6)
 MESH = pl.DeviceIdType.MESH
 HALF_LOG2E = 0.5 * math.log2(math.e)
 TWO_PI = 6.283185307179586
@@ -48,7 +49,7 @@
     mode_ref, var_ref, weight_hbm, grid_hbm,
     density_ref, moments_ref, last_u, last_v, last_c, grid_col,
     stage, relay, landed, weights, norm, weight_ref, grid_ref, rows_u, rows_v, rows_c,
-    small_sem, go_sem, rest_sem, load_sem, pass_sem, relay_sem, send_sem, recv_sem, wsend_sem, wrecv_sem,
+    small_sem, peer_sem, go_sem, rest_sem, pace_sem, load_sem, pass_sem, relay_sem, send_sem, recv_sem, wsend_sem, wrecv_sem,
 ):
     my_cfg = lax.axis_index("cfg")
     my_lat = lax.axis_index("lat")
@@ -70,15 +71,18 @@
     is_gate = core == gate
 
     for step in range(1, n_group):
-        peer = lax.rem(group + step, n_group) * CORES + core
+        peer = lax.rem(group + step, n_group) * CORES + jnp.where(half == 0, 0, core)
         pl.semaphore_signal(
             barrier, inc=1, device_id=(my_cfg, peer), device_id_type=MESH
         )
 
     def greet(i, carry):
         early = i < half_cfg
-        mate = jnp.logical_and(i == my_cfg, core != gate)
+        mate = jnp.logical_and(i == my_cfg, jnp.logical_and(core != gate, half == 1))
         others = jnp.logical_and(i != my_cfg, jnp.logical_or(early, half == 0))
+        mate = jnp.logical_or(
+            mate, jnp.logical_and(i == my_cfg, jnp.logical_and(half == 0, core == 0))
+        )
 
         @pl.when(jnp.logical_or(mate, others))
         def _():
@@ -87,6 +91,12 @@
                 device_id=(i, group * CORES + jnp.where(early, 1, 0)), device_id_type=MESH,
             )
         return carry
+
+    @pl.when(jnp.logical_and(half == 0, core == 1))
+    def _():
+        pl.semaphore_signal(
+            barrier, inc=1, device_id=(my_cfg, group * CORES), device_id_type=MESH
+        )
 
     over(n_cfg, greet, 0)
 
@@ -109,22 +119,25 @@
         copy.start()
 
     peers = n_group - 1
-    gathered = jnp.where(half == 0, n_cfg * CORES - 1, half_cfg * CORES + 1)
-    pl.semaphore_wait(barrier, peers + jnp.where(is_gate, gathered, 0))
-
-    @pl.when(is_gate)
-    def _():
-        pl.semaphore_signal(
-            go_sem, inc=1, device_id=(my_cfg, group * CORES + 1 - gate), device_id_type=MESH
-        )
-
-        @pl.when(half == 0)
+    mate_id = (my_cfg, group * CORES + 1 - core)
+    first_wait = jnp.where(
+        half == 0, peers * CORES + 1,
+        peers + jnp.where(is_gate, half_cfg * CORES + 1, 0),
+    )
+
+    @pl.when(jnp.logical_or(half == 1, core == 0))
+    def _():
+        pl.semaphore_wait(barrier, first_wait)
+
+    @pl.when(half == 0)
+    def _():
+        @pl.when(core == 0)
         def _():
-            for other in range(CORES):
-                pl.semaphore_signal(
-                    rest_sem, inc=1,
-                    device_id=(my_cfg + half_cfg, group * CORES + other), device_id_type=MESH,
-                )
+            pl.semaphore_signal(peer_sem, inc=1, device_id=mate_id, device_id_type=MESH)
+
+        @pl.when(core != 0)
+        def _():
+            pl.semaphore_wait(peer_sem, 1)
 
     def spent(block, sem):
         pltpu.make_async_copy(block, block, sem).wait()
@@ -148,16 +161,28 @@
                 device_id=(my_cfg, to * CORES + core), device_id_type=MESH,
             ).start()
 
-    hops = min(HOPS, n_chunk)
-    for chunk in range(hops):
+    for chunk in range(n_chunk):
         hop(chunk)
 
+    @pl.when(jnp.logical_and(half == 0, is_gate))
+    def _():
+        pl.semaphore_wait(barrier, n_cfg * CORES - 1)
+
+    @pl.when(is_gate)
+    def _():
+        pl.semaphore_signal(go_sem, inc=1, device_id=mate_id, device_id_type=MESH)
+
+        @pl.when(half == 0)
+        def _():
+            for other in range(CORES):
+                pl.semaphore_signal(
+                    rest_sem, inc=1,
+                    device_id=(my_cfg + half_cfg, group * CORES + other), device_id_type=MESH,
+                )
+
     @pl.when(jnp.logical_not(is_gate))
     def _():
         pl.semaphore_wait(go_sem, 1)
-
-    for chunk in range(hops, n_chunk):
-        hop(chunk)
 
     def target(origin, i):
         slot = (i // CORES) * n_lat + group * CORES + i % CORES
@@ -183,7 +208,7 @@
 
         over(per_group, send, 0)
 
-    def send_blocks(origin, source, chunk):
+    def send_blocks(origin, source, chunk, some=None):
         rows = rows_of(chunk)
 
         def send(i, carry):
@@ -204,11 +229,16 @@
                 ).start()
             return carry
 
-        over(per_group, send, 0)
-
-    def send_own(chunk):
-        loaded(0, chunk)
-        send_blocks(group, stage.at[group], chunk)
+        if some is None:
+            over(per_group, send, 0)
+        else:
+            lo, hi = (per_group * p // 2 for p in (some, some + 1))
+            over(hi - lo, lambda i, carry: send(i + lo, carry), 0)
+
+    def send_own(chunk, some=None):
+        if some != 1:
+            loaded(0, chunk)
+        send_blocks(group, stage.at[group], chunk, some)
 
     def crosses(origin):
         return (origin * CORES + core) * 2 // n_lat != half
@@ -235,10 +265,18 @@
     def _():
         weights_where(False)
 
-    @pl.when(jnp.logical_or(half == 0, own_first))
+    @pl.when(half == 0)
     def _():
         for chunk in range(n_chunk):
             send_own(chunk)
+
+    @pl.when(jnp.logical_and(half == 1, own_first))
+    def _():
+        for chunk in range(n_chunk + LEAD):
+            if chunk < n_chunk:
+                send_own(chunk, 0)
+            if chunk >= LEAD:
+                send_own(chunk - LEAD, 1)
 
     ahead = min(AHEAD, n_chunk)
 
@@ -262,8 +300,21 @@
         for chunk in range(ahead):
             send_relayed(chunk)
 
+    relay_crosses = jnp.logical_not(own_first)
     for chunk in range(ahead, n_chunk):
+        for which in range(2):
+            if chunk == HOLD[which]:
+                @pl.when(jnp.logical_and(relay_crosses, jnp.logical_and(half == which, core == 1)))
+                def _():
+                    pl.semaphore_wait(pace_sem, 1)
+
         send_relayed(chunk)
+
+    for which in range(2):
+        if HOLD[which] < n_chunk:
+            @pl.when(jnp.logical_and(relay_crosses, jnp.logical_and(half == which, core == 0)))
+            def _():
+                pl.semaphore_signal(pace_sem, inc=1, device_id=mate_id, device_id_type=MESH)
 
     small[1].wait()
     points = grid_ref.shape[1]
@@ -420,6 +471,8 @@
             dma((2,)),
             pltpu.SemaphoreType.REGULAR,
             pltpu.SemaphoreType.REGULAR,
+            pltpu.SemaphoreType.REGULAR,
+            pltpu.SemaphoreType.REGULAR,
             dma((n_group, 2)),
             dma,
             dma((n_group - 1, n_chunk)),

time: 21.3 us -> 20.6 us (0.967)
  Pallas kernels: 20.5 us -> 19.8 us
    pallas_call x1, Pallas kernels: 19.4 us -> 18.7 us  [per_device(): pl.pallas_call(functools.partial(kernel, n_cfg, n_lat, own, spans), out_s...]
where the time goes in v3:
time: 20.6 us; the launch traced here: 20.4 us
  Pallas kernels  19.8 us (96%)
  between operations  0.64 us (3%)
    pallas_call x1, Pallas kernels, per_device(): pl.pallas_call(functools.partial(kernel, n_cfg, n_lat, own, spans), out_s...  18.7 us
    pallas_call x1, Pallas kernels, per_device(): pl.pallas_call(functools.partial(finish, last), out_shape=(jax.ShapeDtype...  1.14 us

profile of v3, /device:TPU:3, one launch (start us, length us, event | category | flops | bytes accessed | tf_op | source)
XLA Modules:
  0.0 20.4 jit_solution(18020464184186823366)
XLA Ops:
  0.6 18.7 %shard_map.59 = (f32[64,3584]{1,0:T(8,128)S(1)}, f32[64,128]{1,0:T(8,128)S(1)}, f32[16,4,128]{2,1,0:T(4,128)S(1)}, f32[16,4,128]{2,1,0:T(4,128)S(1)}, f32[16,4,128]{2,1,0:T(4,128)S(1)}, /*index=5*/f32[64,128]{1,0:T(8,128)S(1)}) custom-call(f32[2,2,2,64,128]{4,3,2,1,0:T(8,128)} %bitcast.17, f32[2,2,2,64,128]{4,3,2,1,0:T(8,128)} %bitcast.18, f32[1,2]{1,0:T(1,128)} %bitcast.19, ...), custom_call_target="tpu_custom_call" | custom-call | tf_op jit(solution)/shard_map/pallas_call | solution.py:448
  19.3 1.1 %shard_map.60 = (f32[64,4096]{1,0:T(8,128)}, f32[64,128]{1,0:T(8,128)}) custom-call(f32[64,3584]{1,0:T(8,128)S(1)} %get-tuple-element.10.done_ref, f32[64,128]{1,0:T(8,128)S(1)} %get-tuple-element.11.made_ref, f32[16,4,128]{2,1,0:T(4,128)S(1)} %get-tuple-element.12.rows_u, f32[16,4,128]{2,1,0:T(4,128)S(1)} %get-tuple-element.13.rows_v, ...), custom_call_target="tpu_custom_call" | custom-call | tf_op jit(solution)/shard_map/pallas_call | solution.py:491

commit v4 on v3

--- a/solution.py
+++ b/solution.py
@@ -11,7 +11,7 @@
 LANES = 128
 CORES = 2
 UNITS = (1, 1, 1, 1, 1, 1, 1, 1)
-AHEAD = 4
+AHEAD = 6
 LEAD = 4
 HOLD = (8, 6)
 MESH = pl.DeviceIdType.MESH

time: 20.6 us -> 20.5 us (level)
  no operation moved by 1% of the time
where the time goes in v4:
time: 20.5 us; the launch traced here: 20.4 us
  Pallas kernels  19.7 us (96%)
  between operations  0.64 us (3%)
    pallas_call x1, Pallas kernels, per_device(): pl.pallas_call(functools.partial(kernel, n_cfg, n_lat, own, spans), out_s...  18.6 us
    pallas_call x1, Pallas kernels, per_device(): pl.pallas_call(functools.partial(finish, last), out_shape=(jax.ShapeDtype...  1.14 us

profile of v4, /device:TPU:3, one launch (start us, length us, event | category | flops | bytes accessed | tf_op | source)
XLA Modules:
  0.0 20.4 jit_solution(12500442541826767293)
XLA Ops:
  0.6 18.6 %shard_map.59 = (f32[64,3584]{1,0:T(8,128)S(1)}, f32[64,128]{1,0:T(8,128)S(1)}, f32[16,4,128]{2,1,0:T(4,128)S(1)}, f32[16,4,128]{2,1,0:T(4,128)S(1)}, f32[16,4,128]{2,1,0:T(4,128)S(1)}, /*index=5*/f32[64,128]{1,0:T(8,128)S(1)}) custom-call(f32[2,2,2,64,128]{4,3,2,1,0:T(8,128)} %bitcast.17, f32[2,2,2,64,128]{4,3,2,1,0:T(8,128)} %bitcast.18, f32[1,2]{1,0:T(1,128)} %bitcast.19, ...), custom_call_target="tpu_custom_call" | custom-call | tf_op jit(solution)/shard_map/pallas_call | solution.py:448
  19.2 1.1 %shard_map.60 = (f32[64,4096]{1,0:T(8,128)}, f32[64,128]{1,0:T(8,128)}) custom-call(f32[64,3584]{1,0:T(8,128)S(1)} %get-tuple-element.10.done_ref, f32[64,128]{1,0:T(8,128)S(1)} %get-tuple-element.11.made_ref, f32[16,4,128]{2,1,0:T(4,128)S(1)} %get-tuple-element.12.rows_u, f32[16,4,128]{2,1,0:T(4,128)S(1)} %get-tuple-element.13.rows_v, ...), custom_call_target="tpu_custom_call" | custom-call | tf_op jit(solution)/shard_map/pallas_call | solution.py:491
